TPU v7x, 32 devices: a whole 2x2x4 slice. The times are simulated.
32 devices in a mesh: blk: 4 (over x, core), grp: 8 (over z, y).
Axes of the slice: x: 2, y: 2, z: 4, core: 2. Of those that a mesh axis runs over, the one named last changes fastest.
Arguments:
- design: float32 [8, 4096], P(None, ('blk', 'grp')), may hold values from -5 to 5
- lengthscales: float32 [8], replicated, may hold values from 0.55 to 0.85
- counts: int32 [4096], P(('blk', 'grp')), may hold values from 1 to 16
- noise_base: float32 [1], replicated, may hold values from 0.5 to 2
- targets: float32 [16, 4096], P(None, ('blk', 'grp')), may hold values from -6 to 6
Outputs:
- solution: float32 [16, 4096], P(None, ('blk', 'grp'))
- residual: float32 [16, 4096], P(None, ('blk', 'grp'))
- image: float32 [16, 4096], P(None, ('blk', 'grp'))
All inputs are finite; a program needn't handle non-finite values.
Results may differ from a plain program's by a relative error of at most 0.0003.
Values sent between devices are 32-bit elements; how exact they have to be, the bound alone decides.
No kernel may reach another device: no remote copies, remote signals or barrier semaphores. Data moves between devices by JAX's collectives and lax.ppermute only.
A program may use at most 64 MiB of HBM per device.

v0:
```python
import math
import jax
import jax.numpy as jnp
from jax import lax
from jax.sharding import PartitionSpec as P

ROOT_FIVE = 2.23606797749979


def kernel_terms(own_scaled, own_square, col_scaled, col_dirs, running):
    columns = col_scaled.shape[1]
    block_width = math.gcd(columns, 2048)
    block_count = columns // block_width

    def advance(block_index, partial_sum):
        offset = block_index * block_width
        chosen = lax.dynamic_slice_in_dim(col_scaled, offset, block_width, 1)
        chosen_dirs = lax.dynamic_slice_in_dim(col_dirs, offset, block_width, 1)
        chosen_square = jnp.sum(chosen * chosen, 0)
        inner_products = jnp.einsum(
            "dr,dc->rc", own_scaled, chosen, precision=lax.Precision.HIGHEST
        )
        dist_square = jnp.maximum(
            own_square[:, None] + chosen_square[None, :] - 2.0 * inner_products, 0.0
        )
        radius = jnp.sqrt(dist_square)
        kernel_tile = (1.0 + ROOT_FIVE * radius + 5.0 / 3.0 * dist_square) * jnp.exp(
            -ROOT_FIVE * radius
        )
        return partial_sum + jnp.einsum(
            "kc,rc->kr", chosen_dirs, kernel_tile, precision=lax.Precision.HIGHEST
        )

    return lax.fori_loop(0, block_count, advance, running)


def on_device(design, lengthscales, counts, noise_base, targets):
    scaled = design / lengthscales[:, None]
    own_square = jnp.sum(scaled * scaled, 0)
    noise_diag = noise_base[0] / counts.astype(jnp.float32)

    def operator_apply(direction):
        zero_start = jnp.zeros(direction.shape, jnp.float32)
        group_points, group_dirs = (
            lax.all_gather(scaled, "grp", axis=1, tiled=True),
            lax.all_gather(direction, "grp", axis=1, tiled=True),
        )
        product_sum = kernel_terms(
            scaled,
            own_square,
            lax.all_gather(group_points, "blk", axis=1, tiled=True),
            lax.all_gather(group_dirs, "blk", axis=1, tiled=True),
            zero_start,
        )
        return product_sum + noise_diag[None, :] * direction

    first = operator_apply(targets)
    local_gammas = jnp.sum(targets * targets, 1)
    local_deltas = jnp.sum(first * targets, 1)
    gammas, deltas = lax.psum((local_gammas, local_deltas), ("blk", "grp"))
    further = operator_apply(first)
    alphas = (gammas / deltas)[:, None]
    solution = alphas * targets
    residual = targets - alphas * first
    image = first - alphas * further
    return (solution, residual, image)


def solution(mesh):
    in_specs = (P(None, ("blk", "grp")), P(), P(("blk", "grp")), P(), P(None, ("blk", "grp")))
    out_specs = (P(None, ("blk", "grp")), P(None, ("blk", "grp")), P(None, ("blk", "grp")))
    return jax.shard_map(
        on_device, mesh=mesh, in_specs=in_specs, out_specs=out_specs, check_vma=False
    )
```

profile of v0, /device:TPU:0, one launch (start us, length us, event | category | flops | bytes accessed | tf_op | source)
XLA Modules:
  0.0 167.1 jit_solution(15107459266311778984)
XLA Ops:
  0.6 0.0 copy-start.1
  1.3 0.0 copy-start.3
  1.3 0.6 copy-done.3
  2.0 0.6 copy-done.2
  2.6 0.1 multiply_reduce_fusion.4
  2.7 32.6 %all_gather.22 = f32[8,1024]{1,0:T(8,128)S(1)} all-gather(f32[8,128]{1,0:T(8,128)S(1)} %get-tuple-element.408), channel_id=1, replica_groups=mesh['blk'=4,'grp'=8] {'grp'}, dimensions={1}, use_global_device_ids=true | all-gather | bytes 36864 | tf_op jit(solution)/shard_map/all_gather | solution.py:45
  35.3 30.5 %all_gather.20 = f32[16,1024]{1,0:T(8,128)S(1)} all-gather(f32[16,128]{1,0:T(8,128)S(1)} %copy-done), channel_id=1, replica_groups=mesh['blk'=4,'grp'=8] {'grp'}, dimensions={1}, use_global_device_ids=true | all-gather | bytes 73728 | tf_op jit(solution)/shard_map/all_gather | solution.py:46
  65.8 5.4 %all_gather.23 = f32[8,4096]{1,0:T(8,128)S(1)} all-gather(f32[8,1024]{1,0:T(8,128)S(1)} %all_gather.22), channel_id=1, replica_groups=mesh['blk'=4,'grp'=8] {'blk'}, dimensions={1}, use_global_device_ids=true | all-gather | bytes 163840 | tf_op jit(solution)/shard_map/all_gather | solution.py:51
  71.2 5.8 %all_gather.21 = f32[16,4096]{1,0:T(8,128)S(1)} all-gather(f32[16,1024]{1,0:T(8,128)S(1)} %all_gather.20), channel_id=1, replica_groups=mesh['blk'=4,'grp'=8] {'blk'}, dimensions={1}, use_global_device_ids=true | all-gather | bytes 327680 | tf_op jit(solution)/shard_map/all_gather | solution.py:52
  77.0 6.3 %while.28 = (s32[]{:T(128)}, f32[16,128]{1,0:T(8,128)S(1)}, f32[16,4096]{1,0:T(8,128)S(1)}, f32[128]{0:T(128)S(1)}, f32[8,4096]{1,0:T(8,128)S(1)}, /*index=5*/f3...) while((s32[]{:T(128)}, f32[16,128]{1,0:T(8,128)S(1)}, ...), condition=%wide.region_5.0_spmd.clone, body=%wide.region_3.5_spmd.clone.sunk | while | flops 78153728 | bytes 2396849 | solution.py:34
  77.1 2.0 %fusion.62 = f32[128,2048]{0,1:T(8,128)S(1)} fusion(f32[8,128]{1,0:T(8,128)S(1)} %get-tuple-element.398, f32[2048]{0:T(1024)S(1)} %multiply_reduce_fusion.7, f32[128]{0:T(128)S(1)} %get-tuple-element.396, f32[8,4096]{1,0:T(8,128)S(1)} %get-tuple-element.397, s32[]{:T(128)S(6)} %select_n.20), kind=kOutput, calls=%fused_computation.3.clone.1 | convolution fusion | flops 26214400 | bytes 1126916 | tf_op jit(solution)/shard_map/while/body/eval_jaxpr/dr,dc->rc/dot_general | solution.py:20
  79.1 1.1 convolution_add_fusion.4
  80.2 2.0 %fusion.62 = f32[128,2048]{0,1:T(8,128)S(1)} fusion(f32[8,128]{1,0:T(8,128)S(1)} %get-tuple-element.398, f32[2048]{0:T(1024)S(1)} %multiply_reduce_fusion.7, f32[128]{0:T(128)S(1)} %get-tuple-element.396, f32[8,4096]{1,0:T(8,128)S(1)} %get-tuple-element.397, s32[]{:T(128)S(6)} %select_n.20), kind=kOutput, calls=%fused_computation.3.clone.1 | convolution fusion | flops 26214400 | bytes 1126916 | tf_op jit(solution)/shard_map/while/body/eval_jaxpr/dr,dc->rc/dot_general | solution.py:20
  82.2 1.1 convolution_add_fusion.4
  83.4 0.1 multiply_reduce_fusion.2
  83.5 39.5 %all-reduce = (f32[16]{0:T(128)S(1)}, f32[16]{0:T(128)S(1)}) all-reduce(f32[16]{0:T(128)S(1)} %get-tuple-element.266, f32[16]{0:T(128)S(1)} %get-tuple-element.265), channel_id=1, replica_groups=mesh['blk'=4,'grp'=8] {'blk','grp'}, use_global_device_ids=true, to_apply=%region_1.2 | all-reduce | flops 32 | bytes 256 | tf_op jit(solution)/shard_map/psum | solution.py:60
  123.0 30.5 %all_gather.24 = f32[16,1024]{1,0:T(8,128)S(1)} all-gather(f32[16,128]{1,0:T(8,128)S(1)} %get-tuple-element.293), channel_id=1, replica_groups=mesh['blk'=4,'grp'=8] {'grp'}, dimensions={1}, use_global_device_ids=true | all-gather | bytes 73728 | tf_op jit(solution)/shard_map/all_gather | solution.py:46
  153.6 6.5 %all_gather.25 = f32[16,4096]{1,0:T(8,128)S(1)} all-gather(f32[16,1024]{1,0:T(8,128)S(1)} %all_gather.24), channel_id=1, replica_groups=mesh['blk'=4,'grp'=8] {'blk'}, dimensions={1}, use_global_device_ids=true | all-gather | bytes 327680 | tf_op jit(solution)/shard_map/all_gather | solution.py:52
  160.1 6.3 %while.29 = (s32[]{:T(128)}, f32[16,128]{1,0:T(8,128)S(1)}, f32[16,4096]{1,0:T(8,128)S(1)}, f32[128]{0:T(128)S(1)}, f32[8,4096]{1,0:T(8,128)S(1)}, /*index=5*/f3...) while((s32[]{:T(128)}, f32[16,128]{1,0:T(8,128)S(1)}, ...), condition=%wide.region_10.0_spmd.clone, body=%wide.region_8.0_spmd.clone.sunk | while | flops 78153728 | bytes 2396849 | solution.py:34
  160.1 2.0 %fusion.67 = f32[128,2048]{0,1:T(8,128)S(1)} fusion(f32[8,128]{1,0:T(8,128)S(1)} %get-tuple-element.428, f32[2048]{0:T(1024)S(1)} %multiply_reduce_fusion.8, f32[128]{0:T(128)S(1)} %get-tuple-element.426, f32[8,4096]{1,0:T(8,128)S(1)} %get-tuple-element.427, s32[]{:T(128)S(6)} %select_n.21), kind=kOutput, calls=%fused_computation.29.clone.1 | convolution fusion | flops 26214400 | bytes 1126916 | tf_op jit(solution)/shard_map/while/body/eval_jaxpr/dr,dc->rc/dot_general | solution.py:20
  162.1 1.1 convolution_add_fusion.5
  163.3 2.0 %fusion.67 = f32[128,2048]{0,1:T(8,128)S(1)} fusion(f32[8,128]{1,0:T(8,128)S(1)} %get-tuple-element.428, f32[2048]{0:T(1024)S(1)} %multiply_reduce_fusion.8, f32[128]{0:T(128)S(1)} %get-tuple-element.426, f32[8,4096]{1,0:T(8,128)S(1)} %get-tuple-element.427, s32[]{:T(128)S(6)} %select_n.21), kind=kOutput, calls=%fused_computation.29.clone.1 | convolution fusion | flops 26214400 | bytes 1126916 | tf_op jit(solution)/shard_map/while/body/eval_jaxpr/dr,dc->rc/dot_general | solution.py:20
  165.3 1.1 convolution_add_fusion.5
  166.4 0.7 multiply_subtract_fusion
  (12 shorter events, 0.1 us)
Async XLA Ops:
  0.6 1.3 copy-start.1
  1.3 0.7 copy-start.3
  2.0 0.7 copy-start.2
  2.7 32.6 %copy-start = (f32[16,128]{1,0:T(8,128)S(1)}, f32[16,128]{1,0:T(8,128)}, u32[]{:S(2)}) copy-start(f32[16,128]{1,0:T(8,128)} %param.13) | copy-start | bytes 24580
where the time goes:
time: 168 us; the launch traced here: 167 us
  blocking collectives  151 us (90%)
  matrix products  12.4 us (7%)
    all_gather x2, blocking collectives, operator_apply(): lax.all_gather(direction, 'grp', axis=1, tiled=True)  61.1 us
    psum x1, blocking collectives, on_device(): gammas, deltas = lax.psum((local_gammas, local_deltas), ('blk', 'grp'))  39.5 us
    all_gather x1, blocking collectives, operator_apply(): lax.all_gather(scaled, 'grp', axis=1, tiled=True)  32.6 us
    all_gather x2, blocking collectives, operator_apply(): lax.all_gather(group_dirs, 'blk', axis=1, tiled=True)  12.4 us
    dot_general x4, matrix products, advance(): jnp.einsum('dr,dc->rc', own_scaled, chosen, precision=lax.Precision.HIGHEST)  7.95 us
    all_gather x1, blocking collectives, operator_apply(): lax.all_gather(group_points, 'blk', axis=1, tiled=True)  5.4 us
    dot_general x4, matrix products, advance(): jnp.einsum('kc,rc->kr', chosen_dirs, kernel_tile, precision=lax.Precision...  4.49 us

commit v1 on v0

--- a/solution.py
+++ b/solution.py
@@ -49,7 +49,7 @@
             scaled,
             own_square,
             lax.all_gather(group_points, "blk", axis=1, tiled=True),
-            lax.all_gather(group_dirs, "blk", axis=1, tiled=True),
+            jnp.concatenate(lax.all_gather(group_dirs, "blk"), axis=1),
             zero_start,
         )
         return product_sum + noise_diag[None, :] * direction

time: 168 us -> 168 us (level)
  no operation moved by 1% of the time
where the time goes in v1:
time: 168 us
  blocking collectives  151 us (90%)
  matrix products  12.4 us (7%)
    all_gather x2, blocking collectives, operator_apply(): lax.all_gather(direction, 'grp', axis=1, tiled=True)  61.1 us
    psum x1, blocking collectives, on_device(): gammas, deltas = lax.psum((local_gammas, local_deltas), ('blk', 'grp'))  39.5 us
    all_gather x1, blocking collectives, operator_apply(): lax.all_gather(scaled, 'grp', axis=1, tiled=True)  32.6 us
    all_gather x2, blocking collectives, operator_apply(): lax.all_gather(group_dirs, 'blk')  12.4 us
    dot_general x4, matrix products, advance(): jnp.einsum('dr,dc->rc', own_scaled, chosen, precision=lax.Precision.HIGHEST)  7.95 us
    all_gather x1, blocking collectives, operator_apply(): lax.all_gather(group_points, 'blk', axis=1, tiled=True)  5.4 us
    dot_general x4, matrix products, advance(): jnp.einsum('kc,rc->kr', chosen_dirs, kernel_tile, precision=lax.Precision...  4.49 us

profile of v1, /device:TPU:0, one launch (start us, length us, event | category | flops | bytes accessed | tf_op | source)
XLA Modules:
  0.0 167.5 jit_solution(9326192220234191441)
XLA Ops:
  1.3 0.6 copy-done.3
  2.0 0.6 copy-done.2
  2.6 0.1 multiply_reduce_fusion.4
  2.7 32.6 %all_gather.29 = f32[8,1024]{1,0:T(8,128)S(1)} all-gather(f32[8,128]{1,0:T(8,128)S(1)} %get-tuple-element.408), channel_id=1, replica_groups=mesh['blk'=4,'grp'=8] {'grp'}, dimensions={1}, use_global_device_ids=true | all-gather | bytes 36864 | tf_op jit(solution)/shard_map/all_gather | solution.py:45
  35.3 30.5 %all_gather.26 = f32[16,1024]{1,0:T(8,128)S(1)} all-gather(f32[16,128]{1,0:T(8,128)S(1)} %copy-done), channel_id=1, replica_groups=mesh['blk'=4,'grp'=8] {'grp'}, dimensions={1}, use_global_device_ids=true | all-gather | bytes 73728 | tf_op jit(solution)/shard_map/all_gather | solution.py:46
  65.8 5.4 %all_gather.30 = f32[8,4096]{1,0:T(8,128)S(1)} all-gather(f32[8,1024]{1,0:T(8,128)S(1)} %all_gather.29), channel_id=1, replica_groups=mesh['blk'=4,'grp'=8] {'blk'}, dimensions={1}, use_global_device_ids=true | all-gather | bytes 163840 | tf_op jit(solution)/shard_map/all_gather | solution.py:51
  71.2 5.8 %all-gather = f32[64,1024]{1,0:T(8,128)S(1)} all-gather(f32[16,1024]{1,0:T(8,128)S(1)} %all_gather.26), channel_id=2, replica_groups=mesh['blk'=4,'grp'=8] {'blk'}, dimensions={0}, use_global_device_ids=true | all-gather | bytes 327680 | tf_op jit(solution)/shard_map/all_gather | solution.py:52
  77.0 0.2 copy.8
  77.2 0.2 copy.11
  77.4 6.4 %while.28 = (s32[]{:T(128)}, f32[16,128]{1,0:T(8,128)S(1)}, f32[16,4096]{1,0:T(8,128)S(1)}, f32[128]{0:T(128)S(1)}, f32[8,4096]{1,0:T(8,128)S(1)}, /*index=5*/f3...) while((s32[]{:T(128)}, f32[16,128]{1,0:T(8,128)S(1)}, ...), condition=%wide.region_5.0_spmd.clone, body=%wide.region_3.5_spmd.clone.sunk | while | flops 78153728 | bytes 2396849 | solution.py:34
  77.4 2.0 %fusion.62 = f32[128,2048]{0,1:T(8,128)S(1)} fusion(f32[8,128]{1,0:T(8,128)S(1)} %get-tuple-element.398, f32[2048]{0:T(1024)S(1)} %multiply_reduce_fusion.7, f32[128]{0:T(128)S(1)} %get-tuple-element.396, f32[8,4096]{1,0:T(8,128)S(1)} %get-tuple-element.397, s32[]{:T(128)S(6)} %select_n.20), kind=kOutput, calls=%fused_computation.3.clone.1 | convolution fusion | flops 26214400 | bytes 1126916 | tf_op jit(solution)/shard_map/while/body/eval_jaxpr/dr,dc->rc/dot_general | solution.py:20
  79.4 1.1 convolution_add_fusion.4
  80.6 2.0 %fusion.62 = f32[128,2048]{0,1:T(8,128)S(1)} fusion(f32[8,128]{1,0:T(8,128)S(1)} %get-tuple-element.398, f32[2048]{0:T(1024)S(1)} %multiply_reduce_fusion.7, f32[128]{0:T(128)S(1)} %get-tuple-element.396, f32[8,4096]{1,0:T(8,128)S(1)} %get-tuple-element.397, s32[]{:T(128)S(6)} %select_n.20), kind=kOutput, calls=%fused_computation.3.clone.1 | convolution fusion | flops 26214400 | bytes 1126916 | tf_op jit(solution)/shard_map/while/body/eval_jaxpr/dr,dc->rc/dot_general | solution.py:20
  82.6 1.1 convolution_add_fusion.4
  83.7 0.1 multiply_reduce_fusion.2
  83.9 39.5 %all-reduce = (f32[16]{0:T(128)S(1)}, f32[16]{0:T(128)S(1)}) all-reduce(f32[16]{0:T(128)S(1)} %get-tuple-element.266, f32[16]{0:T(128)S(1)} %get-tuple-element.265), channel_id=1, replica_groups=mesh['blk'=4,'grp'=8] {'blk','grp'}, use_global_device_ids=true, to_apply=%region_1.2 | all-reduce | flops 32 | bytes 256 | tf_op jit(solution)/shard_map/psum | solution.py:60
  123.4 30.5 %all_gather.31 = f32[16,1024]{1,0:T(8,128)S(1)} all-gather(f32[16,128]{1,0:T(8,128)S(1)} %get-tuple-element.293), channel_id=1, replica_groups=mesh['blk'=4,'grp'=8] {'grp'}, dimensions={1}, use_global_device_ids=true | all-gather | bytes 73728 | tf_op jit(solution)/shard_map/all_gather | solution.py:46
  153.9 6.5 %all-gather.1 = f32[64,1024]{1,0:T(8,128)S(1)} all-gather(f32[16,1024]{1,0:T(8,128)S(1)} %all_gather.31), channel_id=3, replica_groups=mesh['blk'=4,'grp'=8] {'blk'}, dimensions={0}, use_global_device_ids=true | all-gather | bytes 327680 | tf_op jit(solution)/shard_map/all_gather | solution.py:52
  160.5 6.4 %while.29 = (s32[]{:T(128)}, f32[16,128]{1,0:T(8,128)S(1)}, f32[16,4096]{1,0:T(8,128)S(1)}, f32[128]{0:T(128)S(1)}, f32[8,4096]{1,0:T(8,128)S(1)}, /*index=5*/f3...) while((s32[]{:T(128)}, f32[16,128]{1,0:T(8,128)S(1)}, ...), condition=%wide.region_10.0_spmd.clone, body=%wide.region_8.0_spmd.clone.sunk | while | flops 78153728 | bytes 2396849 | solution.py:34
  160.5 2.0 %fusion.67 = f32[128,2048]{0,1:T(8,128)S(1)} fusion(f32[8,128]{1,0:T(8,128)S(1)} %get-tuple-element.428, f32[2048]{0:T(1024)S(1)} %multiply_reduce_fusion.8, f32[128]{0:T(128)S(1)} %get-tuple-element.426, f32[8,4096]{1,0:T(8,128)S(1)} %get-tuple-element.427, s32[]{:T(128)S(6)} %select_n.21), kind=kOutput, calls=%fused_computation.29.clone.1 | convolution fusion | flops 26214400 | bytes 1126916 | tf_op jit(solution)/shard_map/while/body/eval_jaxpr/dr,dc->rc/dot_general | solution.py:20
  162.5 1.1 convolution_add_fusion.5
  163.7 2.0 %fusion.67 = f32[128,2048]{0,1:T(8,128)S(1)} fusion(f32[8,128]{1,0:T(8,128)S(1)} %get-tuple-element.428, f32[2048]{0:T(1024)S(1)} %multiply_reduce_fusion.8, f32[128]{0:T(128)S(1)} %get-tuple-element.426, f32[8,4096]{1,0:T(8,128)S(1)} %get-tuple-element.427, s32[]{:T(128)S(6)} %select_n.21), kind=kOutput, calls=%fused_computation.29.clone.1 | convolution fusion | flops 26214400 | bytes 1126916 | tf_op jit(solution)/shard_map/while/body/eval_jaxpr/dr,dc->rc/dot_general | solution.py:20
  165.7 1.1 convolution_add_fusion.5
  166.9 0.7 multiply_subtract_fusion
  (15 shorter events, 0.2 us)
Async XLA Ops:
  0.6 1.3 copy-start.1
  1.3 0.7 copy-start.3
  2.0 0.7 copy-start.2
  2.7 32.6 %copy-start = (f32[16,128]{1,0:T(8,128)S(1)}, f32[16,128]{1,0:T(8,128)}, u32[]{:S(2)}) copy-start(f32[16,128]{1,0:T(8,128)} %param.13) | copy-start | bytes 24580
